TPU v7x, 128 devices: a whole 4x4x4 slice. The times are simulated.
128 devices in a mesh: dp: 32 (over x, y, core), mp: 4 (over z).
Axes of the slice: x: 4, y: 4, z: 4, core: 2. Of those that a mesh axis runs over, the one named last changes fastest.
Arguments:
- grad_parts: bfloat16 [32, 4, 1024, 4096], P('dp', None, None, 'mp'), may hold values from -4000 to 4000
- master: float32 [4, 1024, 4096], P(None, 'dp', 'mp'), may hold values from -6 to 6
- first_moment: float32 [4, 1024, 4096], P(None, 'dp', 'mp'), may hold values from -4 to 4
- second_moment: float32 [4, 1024, 4096], P(None, 'dp', 'mp'), may hold values from 0.25 to 4
- left_basis: bfloat16 [4, 1024, 4096], P(None, 'dp', 'mp'), may hold values from -1 to 1, as said below
- right_basis: bfloat16 [4, 1024, 4096], P(None, 'dp', 'mp'), may hold values from -1 to 1, as said below
Outputs:
- weights: bfloat16 [4, 1024, 4096], P(None, None, 'mp')
- new_master: float32 [4, 1024, 4096], P(None, 'dp', 'mp')
- new_first: float32 [4, 1024, 4096], P(None, 'dp', 'mp')
- new_second: float32 [4, 1024, 4096], P(None, 'dp', 'mp')
Inputs may be any that keep to these rules, and one draw needn't show every extreme that they name: Each block left_basis[i, :, j * 1024 : (j + 1) * 1024] is an orthogonal 1024 x 1024 matrix up to rounding. Each block right_basis[i, :, j * 1024 : (j + 1) * 1024] is an orthogonal 1024 x 1024 matrix up to rounding.
All inputs are finite; a program needn't handle non-finite values.
Results may differ from a plain program's by a relative error of at most 0.02.
Values may be sent and summed in bfloat16 or wider, within the bound.
No kernel may reach another device: no remote copies, remote signals or barrier semaphores. Data moves between devices by JAX's collectives and lax.ppermute only.
A program may use at most 128 MiB of HBM per device.

v0:
```python
import jax
import jax.numpy as jnp
from jax import lax
from jax.sharding import Mesh
from jax.sharding import PartitionSpec as P

D = 4096
STEP = 10
DP = ("dp_0", "dp_1", "dp_2")
DP_MP = ("dp_0", "dp_1", "dp_2", "mp")
beta_one = 0.95
beta_two = 0.95
epsilon = 1e-08
norm_epsilon = 1e-06
learning_rate = 0.3
decay_rate = 0.1


def over_axes(array, axes):
    for axis in axes:
        array = lax.psum(array, axis)
    return array


def split_up(array, dim, peers):
    before, after = (array.shape[:dim], array.shape[dim + 1 :])
    return jnp.moveaxis(array.reshape(*before, peers, -1, *after), dim, 0)


def summed_rows(array, chips, core, dim):
    sizes = (lax.axis_size(chips), lax.axis_size(core))
    parts = split_up(array, dim, sizes[0] * sizes[1])
    inside = parts.shape[1:]
    parts = parts.reshape(*sizes, *inside).swapaxes(0, 1).reshape(-1, *inside)
    parts = lax.psum_scatter(parts, core, scatter_dimension=0, tiled=True)
    return lax.psum_scatter(parts, chips, scatter_dimension=0, tiled=True)[0]


def per_device(grad_parts, master, first_moment, second_moment, left_basis, right_basis):
    gradient = lax.psum_scatter(grad_parts[0], DP, scatter_dimension=1, tiled=True).astype(
        jnp.float32
    )
    squares_sum = over_axes(jnp.sum(gradient * gradient), DP_MP)
    clip_scale = jnp.minimum(1.0, 2.0 * D / jnp.sqrt(squares_sum + norm_epsilon))
    grad_low = gradient.astype(jnp.bfloat16)
    right_full = lax.all_gather(right_basis, DP, axis=1, tiled=True)
    turned = jnp.einsum(
        "isk,ikb->isb", grad_low, right_full, preferred_element_type=jnp.float32
    ).astype(jnp.bfloat16)
    left_cols = left_basis
    raw_term = jnp.einsum("isx,isb->xib", left_cols, turned, preferred_element_type=jnp.float32)
    rotated_rows = summed_rows(
        lax.optimization_barrier(raw_term.astype(jnp.bfloat16))
        .astype(jnp.float32)
        .astype(jnp.bfloat16),
        ("dp_0", "dp_1"),
        "dp_2",
        0,
    ).astype(jnp.float32)
    rotated = jnp.transpose(rotated_rows, (1, 0, 2))
    clipped = clip_scale * rotated
    new_first = beta_one * first_moment + (1.0 - beta_one) * clipped
    new_second = beta_two * second_moment + (1.0 - beta_two) * clipped * clipped
    bias_one = 1.0 - beta_one**STEP
    bias_two = 1.0 - beta_two**STEP
    direction = (new_first / bias_one / (jnp.sqrt(new_second / bias_two) + epsilon)).astype(
        jnp.bfloat16
    )
    back_rows = jnp.einsum(
        "isb,icb->isc", direction, right_full, preferred_element_type=jnp.float32
    ).astype(jnp.bfloat16)
    left_cols = left_basis
    update = jnp.einsum(
        "isk,ikc->isc",
        left_cols,
        lax.all_gather(back_rows, DP, axis=1, tiled=True),
        preferred_element_type=jnp.float32,
    )
    new_master = master * (1.0 - learning_rate * decay_rate) - learning_rate * update
    weights = lax.all_gather(new_master.astype(jnp.bfloat16), DP, axis=1, tiled=True)
    return (weights, new_master, new_first, new_second)


def solution(mesh):
    finer = Mesh(mesh.devices.reshape(4, 4, 2, mesh.shape["mp"]), ("dp_0", "dp_1", "dp_2", "mp"))
    placed = (
        P(DP, None, None, "mp"),
        P(None, DP, "mp"),
        P(None, DP, "mp"),
        P(None, DP, "mp"),
        P(None, DP, "mp"),
        P(None, DP, "mp"),
    )
    return jax.shard_map(
        per_device,
        mesh=finer,
        in_specs=placed,
        out_specs=(P(None, None, "mp"), P(None, DP, "mp"), P(None, DP, "mp"), P(None, DP, "mp")),
        check_vma=False,
    )
```

profile of v0, /device:TPU:1, one launch (start us, length us, event | category | flops | bytes accessed | tf_op | source)
XLA Modules:
  0.0 428.3 jit_solution(16834403755977702970)
XLA Ops:
  7.2 0.0 copy-start
  7.2 0.0 reduce-scatter.6.cloned.1.call-start
  7.2 0.7 reduce-scatter.6.cloned.1.call-update
  7.9 0.0 all-gather.4.cloned.1.call-start
  8.0 0.7 all-gather.4.cloned.1.call-update
  8.7 0.0 reduce-scatter.8.cloned.1.call-start
  8.7 97.1 %reduce-scatter.6.cloned.1.call-done = bf16[4,32,1024]{2,1,0:T(8,128)(2,1)} async-done(((bf16[4,1024,1024]{2,1,0:T(8,128)(2,1)}), bf16[4,32,1024]{2,1,0:T(8,128)(2,1)}) %reduce-scatter.6.cloned.1.call-update) | async-done | bytes 262160 | tf_op jit(solution)/shard_map/reduce_scatter | solution.py:40
  105.8 56.5 %all-gather.4.cloned.1.call-done = bf16[4,1024,1024]{2,1,0:T(8,128)(2,1)} async-done(((bf16[4,32,1024]{2,1,0:T(8,128)(2,1)}), bf16[4,1024,1024]{2,1,0:T(8,128)(2,1)}) %all-gather.4.cloned.1.call-update) | async-done | bytes 8388624 | tf_op jit(solution)/shard_map/all_gather | solution.py:46
  162.3 0.0 copy-done
  162.3 10.8 %convert_bitcast_fusion = bf16[1024,4,1024]{0,2,1:T(8,128)(2,1)} fusion(bf16[4,32,1024]{2,1,0:T(8,128)(2,1)S(1)} %copy-done, bf16[4,32,1024]{2,1,0:T(8,128)(2,1)} %reduce-scatter.6.cloned.1.call-done, bf16[4,1024,1024]{2,1,0:T(8,128)(2,1)} %all-gather.4.cloned.1.call-done), kind=kOutput, calls=%fused_computation | convolution fusion | flops 541196288 | bytes 17301504 | tf_op jit(solution)/shard_map/isx,isb->xib/dot_general | solution.py:51
  173.2 11.4 %copy.14 = bf16[1024,4,1024]{2,0,1:T(8,128)(2,1)} copy(bf16[1024,4,1024]{0,2,1:T(8,128)(2,1)} %convert_bitcast_fusion) | data formatting | bytes 16777216 | tf_op jit(solution)/shard_map/optimization_barrier | solution.py:53
  184.6 8.6 %copy.15 = bf16[2,16,32,4,1024]{4,2,3,1,0:T(8,128)(2,1)} copy(bf16[2,16,32,4,1024]{4,2,0,1,3:T(8,128)(2,1)} %bitcast.24) | data formatting | bytes 16777216 | tf_op jit(solution)/shard_map/transpose | solution.py:34
  193.2 0.0 copy-start.3
  193.2 0.0 copy-start.4
  193.2 0.0 copy-start.5
  193.2 0.0 reduce-scatter.8.cloned.1.call-update
  193.3 0.0 reduce-scatter.10.cloned.1.call-start
  193.3 18.8 %reduce-scatter.8.cloned.1.call-done = bf16[16,32,4,1024]{3,1,2,0:T(8,128)(2,1)} async-done(((bf16[32,32,4,1024]{3,1,2,0:T(8,128)(2,1)}), bf16[16,32,4,1024]{3,1,2,0:T(8,128)(2,1)}) %reduce-scatter.8.cloned.1.call-update) | async-done | bytes 4194320 | tf_op jit(solution)/shard_map/reduce_scatter | solution.py:35
  212.1 0.0 copy-start.6
  212.1 0.0 reduce-scatter.10.cloned.1.call-update
  212.1 0.0 all-gather.6.cloned.1.call-start
  212.2 0.0 copy-done.3
  212.2 0.7 multiply_reduce_fusion
  212.9 9.1 %psum.28 = f32[]{:T(128)} all-reduce(f32[]{:T(128)} %multiply_reduce_fusion), channel_id=1, replica_groups=mesh['dp_0'=4,'dp_1'=4,'dp_2'=2,'mp'=4] {'dp_0'}, use_global_device_ids=true, to_apply=%region_2.0 | all-reduce | flops 1 | bytes 8 | tf_op jit(solution)/shard_map/psum | solution.py:21
  222.0 9.5 %psum.29 = f32[]{:T(128)} all-reduce(f32[]{:T(128)} %psum.28), channel_id=1, replica_groups=mesh['dp_0'=4,'dp_1'=4,'dp_2'=2,'mp'=4] {'dp_1'}, use_global_device_ids=true, to_apply=%region_3.0 | all-reduce | flops 1 | bytes 8 | tf_op jit(solution)/shard_map/psum | solution.py:21
  231.5 6.7 %psum.30 = f32[]{:T(128)} all-reduce(f32[]{:T(128)} %psum.29), channel_id=1, replica_groups=mesh['dp_0'=4,'dp_1'=4,'dp_2'=2,'mp'=4] {'dp_2'}, use_global_device_ids=true, to_apply=%region_4.0 | all-reduce | flops 1 | bytes 8 | tf_op jit(solution)/shard_map/psum | solution.py:21
  238.2 9.5 %psum.31 = f32[]{:T(128)} all-reduce(f32[]{:T(128)} %psum.30), channel_id=1, replica_groups=mesh['dp_0'=4,'dp_1'=4,'dp_2'=2,'mp'=4] {'mp'}, use_global_device_ids=true, to_apply=%region_5.0 | all-reduce | flops 1 | bytes 8 | tf_op jit(solution)/shard_map/psum | solution.py:21
  248.4 44.5 %reduce-scatter.10.cloned.1.call-done = bf16[1,32,4,1024]{3,1,2,0:T(8,128)(2,1)} async-done(((bf16[16,32,4,1024]{3,1,2,0:T(8,128)(2,1)}), bf16[1,32,4,1024]{3,1,2,0:T(8,128)(2,1)}) %reduce-scatter.10.cloned.1.call-update) | async-done | bytes 262160
  292.9 0.0 copy-done.4
  292.9 0.0 copy-done.5
  293.0 1.1 multiply_add_fusion
  294.1 0.0 copy-start.1
  294.1 0.0 copy-start.2
  294.1 7.0 %convolution_convert_fusion = bf16[4,32,1024]{2,1,0:T(8,128)(2,1)} fusion(bf16[4,1024,1024]{2,1,0:T(8,128)(2,1)} %all-gather.4.cloned.1.call-done, f32[4,32,1024]{2,1,0:T(8,128)S(1)} %get-tuple-element.15, f32[4,32,1024]{2,1,0:T(8,128)S(1)} %get-tuple-element.14), kind=kOutput, calls=%fused_computation.4 | convolution fusion | flops 269221888 | bytes 9699328 | tf_op jit(solution)/shard_map/isb,icb->isc/dot_general | solution.py:69
  301.2 0.0 all-gather.6.cloned.1.call-update
  301.2 0.0 all-gather.8.cloned.1.call-start
  301.2 54.2 %all-gather.6.cloned.1.call-done = bf16[4,1024,1024]{2,1,0:T(8,128)(2,1)} async-done(((bf16[4,32,1024]{2,1,0:T(8,128)(2,1)}), bf16[4,1024,1024]{2,1,0:T(8,128)(2,1)}) %all-gather.6.cloned.1.call-update) | async-done | bytes 8388624 | tf_op jit(solution)/shard_map/all_gather | solution.py:76
  355.4 0.0 copy-done.6
  355.4 5.8 %fusion.7 = (bf16[4,32,1024]{2,1,0:T(8,128)(2,1)}, f32[4,32,1024]{2,1,0:T(8,128)}) fusion(bf16[4,32,1024]{2,1,0:T(8,128)(2,1)S(1)} %copy-done, bf16[4,1024,1024]{2,1,0:T(8,128)(2,1)} %all-gather.6.cloned.1.call-done, f32[4,32,1024]{2,1,0:T(8,128)S(1)} %copy-done.6), kind=kOutput, calls=%fused_computation.16 | convolution fusion | flops 268959744 | bytes 9961472 | tf_op jit(solution)/shard_map/isk,ikc->isc/dot_general | solution.py:73
  361.2 0.0 copy-done.1
  361.2 0.0 copy-done.2
  361.2 0.0 all-gather.8.cloned.1.call-update
  361.3 52.4 %all-gather.8.cloned.1.call-done = bf16[4,1024,1024]{2,1,0:T(8,128)(2,1)} async-done(((bf16[4,32,1024]{2,1,0:T(8,128)(2,1)}), bf16[4,1024,1024]{2,1,0:T(8,128)(2,1)}) %all-gather.8.cloned.1.call-update) | async-done | bytes 8388624 | tf_op jit(solution)/shard_map/all_gather | solution.py:80
  413.7 7.8 %copy.17 = bf16[4,1024,1024]{2,1,0:T(8,128)(2,1)} copy(bf16[4,1024,1024]{2,1,0:T(8,128)(2,1)} %all-gather.8.cloned.1.call-done) | data formatting | bytes 16777216
Async XLA Ops:
  7.2 155.2 %copy-start = (bf16[4,32,1024]{2,1,0:T(8,128)(2,1)S(1)}, bf16[4,32,1024]{2,1,0:T(8,128)(2,1)}, u32[]{:S(2)}) copy-start(bf16[4,32,1024]{2,1,0:T(8,128)(2,1)} %param.10) | copy-start | bytes 786436
  7.2 98.6 %reduce-scatter.6.cloned.1.call-start = ((), (), s32[]{:S(2)}) async-start(), calls=%async_computation.3 | async-start | bytes 8650752 | tf_op jit(solution)/shard_map/reduce_scatter | solution.py:40
  7.9 154.4 %all-gather.4.cloned.1.call-start = ((), (), s32[]{:S(2)}) async-start(), calls=%async_computation.4 | async-start | bytes 8650752 | tf_op jit(solution)/shard_map/all_gather | solution.py:46
  8.7 203.4 %reduce-scatter.8.cloned.1.call-start = ((), (), s32[]{:S(2)}) async-start(), calls=%async_computation.5 | async-start | bytes 12582912 | tf_op jit(solution)/shard_map/reduce_scatter | solution.py:35
  193.2 19.0 %copy-start.3 = (bf16[4,32,1024]{2,1,0:T(8,128)(2,1)S(1)}, bf16[4,32,1024]{2,1,0:T(8,128)(2,1)}, u32[]{:S(2)}) copy-start(bf16[4,32,1024]{2,1,0:T(8,128)(2,1)} %reduce-scatter.6.cloned.1.call-done) | copy-start | bytes 786436
  193.2 99.7 %copy-start.4 = (f32[4,32,1024]{2,1,0:T(8,128)S(1)}, f32[4,32,1024]{2,1,0:T(8,128)}, u32[]{:S(2)}) copy-start(f32[4,32,1024]{2,1,0:T(8,128)} %param.8) | copy-start | bytes 1572868
  193.2 99.7 %copy-start.5 = (f32[4,32,1024]{2,1,0:T(8,128)S(1)}, f32[4,32,1024]{2,1,0:T(8,128)}, u32[]{:S(2)}) copy-start(f32[4,32,1024]{2,1,0:T(8,128)} %param.9) | copy-start | bytes 1572868
  193.3 99.7 %reduce-scatter.10.cloned.1.call-start = ((), (), s32[]{:S(2)}) async-start(), calls=%async_computation.8 | async-start | bytes 4456448
  212.1 143.3 %copy-start.6 = (f32[4,32,1024]{2,1,0:T(8,128)S(1)}, f32[4,32,1024]{2,1,0:T(8,128)}, u32[]{:S(2)}) copy-start(f32[4,32,1024]{2,1,0:T(8,128)} %param.7) | copy-start | bytes 1572868
  212.1 143.3 %all-gather.6.cloned.1.call-start = ((), (), s32[]{:S(2)}) async-start(), calls=%async_computation.6 | async-start | bytes 8650752 | tf_op jit(solution)/shard_map/all_gather | solution.py:76
  294.1 67.1 %copy-start.1 = (f32[4,32,1024]{2,1,0:T(8,128)}, f32[4,32,1024]{2,1,0:T(8,128)S(1)}, u32[]{:S(2)}) copy-start(f32[4,32,1024]{2,1,0:T(8,128)S(1)} %get-tuple-element.14) | copy-start | bytes 1572868
  294.1 67.1 %copy-start.2 = (f32[4,32,1024]{2,1,0:T(8,128)}, f32[4,32,1024]{2,1,0:T(8,128)S(1)}, u32[]{:S(2)}) copy-start(f32[4,32,1024]{2,1,0:T(8,128)S(1)} %get-tuple-element.15) | copy-start | bytes 1572868
  301.2 112.5 %all-gather.8.cloned.1.call-start = ((), (), s32[]{:S(2)}) async-start(), calls=%async_computation.7 | async-start | bytes 8650752 | tf_op jit(solution)/shard_map/all_gather | solution.py:80
Sparse Core Ops, SparseCore 0:
  11.7 94.0 reduce-scatter.5
  108.2 54.1 all-gather.3
  193.4 18.6 reduce-scatter.7
  215.3 77.5 reduce-scatter.9
  301.3 54.0 all-gather.5
  361.4 52.2 all-gather.7
where the time goes:
time: 429 us; the launch traced here: 428 us
  waiting for transfers between devices  325 us (76%)
  blocking collectives  34.8 us (8%)
  local copies, waits for them, and re-layouts  27.8 us (6%)
  matrix products  23.7 us (6%)
  between operations  14.9 us (3%)
    reduce_scatter x1, waiting for transfers between devices, per_device(): lax.psum_scatter(grad_parts[0], DP, scatter_dimension=1, tiled=True)  97.1 us
    all_gather x1, waiting for transfers between devices, per_device(): right_full = lax.all_gather(right_basis, DP, axis=1, tiled=True)  56.5 us
    all_gather x1, waiting for transfers between devices, per_device(): lax.all_gather(back_rows, DP, axis=1, tiled=True)  54.2 us
    all_gather x1, waiting for transfers between devices, per_device(): lax.all_gather(new_master.astype(jnp.bfloat16), DP, axis=1, tiled=True)  52.4 us
    unnamed x7, waiting for transfers between devices  46 us
    psum x4, blocking collectives, over_axes(): array = lax.psum(array, axis)  34.8 us
    reduce_scatter x1, waiting for transfers between devices, summed_rows(): parts = lax.psum_scatter(parts, core, scatter_dimension=0, tiled=True)  18.8 us
    optimization_barrier x1, local copies, waits for them, and re-layouts, per_device(): lax.optimization_barrier(raw_term.astype(jnp.bfloat16)).astype(jnp.float32)  11.4 us
  transfers between devices with their start and end apart: 6, of which 6 were waited for; matrix products, arithmetic and copies ran while one was open for 0% of the time, Pallas kernels for 0%

commit v1 on v0

--- a/solution.py
+++ b/solution.py
@@ -77,7 +77,10 @@
         preferred_element_type=jnp.float32,
     )
     new_master = master * (1.0 - learning_rate * decay_rate) - learning_rate * update
-    weights = lax.all_gather(new_master.astype(jnp.bfloat16), DP, axis=1, tiled=True)
+    weights = jnp.concatenate(
+        lax.all_to_all(jnp.stack([new_master.astype(jnp.bfloat16)] * lax.axis_size(DP)), DP, 0, 0),
+        axis=1,
+    )
     return (weights, new_master, new_first, new_second)
 
 

time: 429 us -> 479 us (1.12)
  blocking collectives: 34.8 us -> 136 us
  waiting for transfers between devices: 325 us -> 273 us
    all_to_all x0 -> x1, blocking collectives: none -> 101 us  [per_device(): lax.all_to_all(jnp.stack([new_master.astype(jnp.bfloat16)] * lax.axis_siz...]
    all_gather x1 -> x0, waiting for transfers between devices: 52.4 us -> none  [per_device(): lax.all_gather(new_master.astype(jnp.bfloat16), DP, axis=1, tiled=True)]
    all_to_all x0 -> x1, local copies, waits for them, and re-layouts: none -> 8.64 us  [per_device(): lax.all_to_all(jnp.stack([new_master.astype(jnp.bfloat16)] * lax.axis_siz...]
    unnamed x15 -> x14, local copies, waits for them, and re-layouts: 7.79 us -> 0.04 us
    unnamed x7 -> x6, waiting for transfers between devices: 46 us -> 46 us
  transfers between devices with their start and end apart: 6 -> 5, of which waited for: 6 -> 5; matrix products, arithmetic and copies ran while one was open for 0% -> 0% of each run, Pallas kernels for 0% -> 0%
where the time goes in v1:
time: 479 us; the launch traced here: 478 us
  waiting for transfers between devices  273 us (57%)
  blocking collectives  136 us (28%)
  local copies, waits for them, and re-layouts  29.8 us (6%)
  matrix products  23.6 us (5%)
  between operations  14.5 us (3%)
    all_to_all x1, blocking collectives, per_device(): lax.all_to_all(jnp.stack([new_master.astype(jnp.bfloat16)] * lax.axis_siz...  101 us
    reduce_scatter x1, waiting for transfers between devices, per_device(): lax.psum_scatter(grad_parts[0], DP, scatter_dimension=1, tiled=True)  97.1 us
    all_gather x1, waiting for transfers between devices, per_device(): right_full = lax.all_gather(right_basis, DP, axis=1, tiled=True)  56.5 us
    all_gather x1, waiting for transfers between devices, per_device(): lax.all_gather(back_rows, DP, axis=1, tiled=True)  54.2 us
    unnamed x6, waiting for transfers between devices  46 us
    psum x4, blocking collectives, over_axes(): array = lax.psum(array, axis)  34.8 us
    reduce_scatter x1, waiting for transfers between devices, summed_rows(): parts = lax.psum_scatter(parts, core, scatter_dimension=0, tiled=True)  18.8 us
    optimization_barrier x1, local copies, waits for them, and re-layouts, per_device(): lax.optimization_barrier(raw_term.astype(jnp.bfloat16)).astype(jnp.float32)  11.4 us
  transfers between devices with their start and end apart: 5, of which 5 were waited for; matrix products, arithmetic and copies ran while one was open for 0% of the time, Pallas kernels for 0%

profile of v1, /device:TPU:1, one launch (start us, length us, event | category | flops | bytes accessed | tf_op | source)
XLA Modules:
  0.0 478.3 jit_solution(9779430416640744740)
XLA Ops:
  7.2 0.0 copy-start
  7.2 0.0 reduce-scatter.6.cloned.1.call-start
  7.2 0.7 reduce-scatter.6.cloned.1.call-update
  7.9 0.0 all-gather.3.cloned.1.call-start
  8.0 0.7 all-gather.3.cloned.1.call-update
  8.7 0.0 reduce-scatter.8.cloned.1.call-start
  8.7 97.1 %reduce-scatter.6.cloned.1.call-done = bf16[4,32,1024]{2,1,0:T(8,128)(2,1)} async-done(((bf16[4,1024,1024]{2,1,0:T(8,128)(2,1)}), bf16[4,32,1024]{2,1,0:T(8,128)(2,1)}) %reduce-scatter.6.cloned.1.call-update) | async-done | bytes 262160 | tf_op jit(solution)/shard_map/reduce_scatter | solution.py:40
  105.8 56.5 %all-gather.3.cloned.1.call-done = bf16[4,1024,1024]{2,1,0:T(8,128)(2,1)} async-done(((bf16[4,32,1024]{2,1,0:T(8,128)(2,1)}), bf16[4,1024,1024]{2,1,0:T(8,128)(2,1)}) %all-gather.3.cloned.1.call-update) | async-done | bytes 8388624 | tf_op jit(solution)/shard_map/all_gather | solution.py:46
  162.3 0.0 copy-done
  162.3 10.8 %convert_bitcast_fusion = bf16[1024,4,1024]{0,2,1:T(8,128)(2,1)} fusion(bf16[4,32,1024]{2,1,0:T(8,128)(2,1)S(1)} %copy-done, bf16[4,32,1024]{2,1,0:T(8,128)(2,1)} %reduce-scatter.6.cloned.1.call-done, bf16[4,1024,1024]{2,1,0:T(8,128)(2,1)} %all-gather.3.cloned.1.call-done), kind=kOutput, calls=%fused_computation | convolution fusion | flops 541196288 | bytes 17301504 | tf_op jit(solution)/shard_map/isx,isb->xib/dot_general | solution.py:51
  173.2 11.4 %copy.16 = bf16[1024,4,1024]{2,0,1:T(8,128)(2,1)} copy(bf16[1024,4,1024]{0,2,1:T(8,128)(2,1)} %convert_bitcast_fusion) | data formatting | bytes 16777216 | tf_op jit(solution)/shard_map/optimization_barrier | solution.py:53
  184.6 8.6 %copy.17 = bf16[2,16,32,4,1024]{4,2,3,1,0:T(8,128)(2,1)} copy(bf16[2,16,32,4,1024]{4,2,0,1,3:T(8,128)(2,1)} %bitcast.27) | data formatting | bytes 16777216 | tf_op jit(solution)/shard_map/transpose | solution.py:34
  193.2 0.0 copy-start.3
  193.2 0.0 copy-start.4
  193.2 0.0 copy-start.5
  193.2 0.0 reduce-scatter.8.cloned.1.call-update
  193.2 0.0 reduce-scatter.10.cloned.1.call-start
  193.3 18.8 %reduce-scatter.8.cloned.1.call-done = bf16[16,32,4,1024]{3,1,2,0:T(8,128)(2,1)} async-done(((bf16[32,32,4,1024]{3,1,2,0:T(8,128)(2,1)}), bf16[16,32,4,1024]{3,1,2,0:T(8,128)(2,1)}) %reduce-scatter.8.cloned.1.call-update) | async-done | bytes 4194320 | tf_op jit(solution)/shard_map/reduce_scatter | solution.py:35
  212.1 0.0 copy-start.6
  212.1 0.0 reduce-scatter.10.cloned.1.call-update
  212.1 0.0 all-gather.5.cloned.1.call-start
  212.2 0.0 copy-done.3
  212.2 0.7 multiply_reduce_fusion
  212.9 9.1 %psum.28 = f32[]{:T(128)} all-reduce(f32[]{:T(128)} %multiply_reduce_fusion), channel_id=1, replica_groups=mesh['dp_0'=4,'dp_1'=4,'dp_2'=2,'mp'=4] {'dp_0'}, use_global_device_ids=true, to_apply=%region_2.0 | all-reduce | flops 1 | bytes 8 | tf_op jit(solution)/shard_map/psum | solution.py:21
  222.0 9.5 %psum.29 = f32[]{:T(128)} all-reduce(f32[]{:T(128)} %psum.28), channel_id=1, replica_groups=mesh['dp_0'=4,'dp_1'=4,'dp_2'=2,'mp'=4] {'dp_1'}, use_global_device_ids=true, to_apply=%region_3.0 | all-reduce | flops 1 | bytes 8 | tf_op jit(solution)/shard_map/psum | solution.py:21
  231.5 6.7 %psum.30 = f32[]{:T(128)} all-reduce(f32[]{:T(128)} %psum.29), channel_id=1, replica_groups=mesh['dp_0'=4,'dp_1'=4,'dp_2'=2,'mp'=4] {'dp_2'}, use_global_device_ids=true, to_apply=%region_4.0 | all-reduce | flops 1 | bytes 8 | tf_op jit(solution)/shard_map/psum | solution.py:21
  238.2 9.5 %psum.31 = f32[]{:T(128)} all-reduce(f32[]{:T(128)} %psum.30), channel_id=1, replica_groups=mesh['dp_0'=4,'dp_1'=4,'dp_2'=2,'mp'=4] {'mp'}, use_global_device_ids=true, to_apply=%region_5.0 | all-reduce | flops 1 | bytes 8 | tf_op jit(solution)/shard_map/psum | solution.py:21
  248.4 44.5 %reduce-scatter.10.cloned.1.call-done = bf16[1,32,4,1024]{3,1,2,0:T(8,128)(2,1)} async-done(((bf16[16,32,4,1024]{3,1,2,0:T(8,128)(2,1)}), bf16[1,32,4,1024]{3,1,2,0:T(8,128)(2,1)}) %reduce-scatter.10.cloned.1.call-update) | async-done | bytes 262160
  292.9 0.0 copy-done.4
  292.9 0.0 copy-done.5
  292.9 1.1 multiply_add_fusion
  294.1 0.0 copy-start.1
  294.1 0.0 copy-start.2
  294.1 7.0 %convolution_convert_fusion = bf16[4,32,1024]{2,1,0:T(8,128)(2,1)} fusion(bf16[4,1024,1024]{2,1,0:T(8,128)(2,1)} %all-gather.3.cloned.1.call-done, f32[4,32,1024]{2,1,0:T(8,128)S(1)} %get-tuple-element.5, f32[4,32,1024]{2,1,0:T(8,128)S(1)} %get-tuple-element.4), kind=kOutput, calls=%fused_computation.4 | convolution fusion | flops 269221888 | bytes 9699328 | tf_op jit(solution)/shard_map/isb,icb->isc/dot_general | solution.py:69
  301.2 0.0 all-gather.5.cloned.1.call-update
  301.2 54.2 %all-gather.5.cloned.1.call-done = bf16[4,1024,1024]{2,1,0:T(8,128)(2,1)} async-done(((bf16[4,32,1024]{2,1,0:T(8,128)(2,1)}), bf16[4,1024,1024]{2,1,0:T(8,128)(2,1)}) %all-gather.5.cloned.1.call-update) | async-done | bytes 8388624 | tf_op jit(solution)/shard_map/all_gather | solution.py:76
  355.4 0.0 copy-done.6
  355.4 5.7 %fusion.7 = (bf16[4,32,1024]{2,1,0:T(8,128)(2,1)S(1)}, f32[4,32,1024]{2,1,0:T(8,128)}) fusion(bf16[4,32,1024]{2,1,0:T(8,128)(2,1)S(1)} %copy-done, bf16[4,1024,1024]{2,1,0:T(8,128)(2,1)} %all-gather.5.cloned.1.call-done, f32[4,32,1024]{2,1,0:T(8,128)S(1)} %copy-done.6), kind=kOutput, calls=%fused_computation.16 | convolution fusion | flops 268959744 | bytes 9961472 | tf_op jit(solution)/shard_map/isk,ikc->isc/dot_general | solution.py:73
  361.1 0.0 copy-done.1
  361.1 0.0 copy-done.2
  361.2 1.1 stack.2
  362.2 100.9 %all_to_all.5 = bf16[32,4,32,1024]{3,2,1,0:T(8,128)(2,1)} all-to-all(bf16[32,4,32,1024]{3,2,1,0:T(8,128)(2,1)S(1)} %stack.2), channel_id=1, replica_groups=mesh['dp_0'=4,'dp_1'=4,'dp_2'=2,'mp'=4] {'dp_0','dp_1','dp_2'}, dimensions={0} | all-to-all | bytes 16777216 | tf_op jit(solution)/shard_map/all_to_all | solution.py:81
  463.2 8.6 %copy.18 = bf16[32,4,32,1024]{3,2,0,1:T(8,128)(2,1)} copy(bf16[32,4,32,1024]{3,2,1,0:T(8,128)(2,1)} %all_to_all.5) | data formatting | bytes 16777216 | tf_op jit(solution)/shard_map/all_to_all | solution.py:81
Async XLA Ops:
  7.2 155.2 %copy-start = (bf16[4,32,1024]{2,1,0:T(8,128)(2,1)S(1)}, bf16[4,32,1024]{2,1,0:T(8,128)(2,1)}, u32[]{:S(2)}) copy-start(bf16[4,32,1024]{2,1,0:T(8,128)(2,1)} %param.10) | copy-start | bytes 786436
  7.2 98.6 %reduce-scatter.6.cloned.1.call-start = ((), (), s32[]{:S(2)}) async-start(), calls=%async_computation.4 | async-start | bytes 8650752 | tf_op jit(solution)/shard_map/reduce_scatter | solution.py:40
  7.9 154.4 %all-gather.3.cloned.1.call-start = ((), (), s32[]{:S(2)}) async-start(), calls=%async_computation.5 | async-start | bytes 8650752 | tf_op jit(solution)/shard_map/all_gather | solution.py:46
  8.7 203.4 %reduce-scatter.8.cloned.1.call-start = ((), (), s32[]{:S(2)}) async-start(), calls=%async_computation.6 | async-start | bytes 12582912 | tf_op jit(solution)/shard_map/reduce_scatter | solution.py:35
  193.2 19.0 %copy-start.3 = (bf16[4,32,1024]{2,1,0:T(8,128)(2,1)S(1)}, bf16[4,32,1024]{2,1,0:T(8,128)(2,1)}, u32[]{:S(2)}) copy-start(bf16[4,32,1024]{2,1,0:T(8,128)(2,1)} %reduce-scatter.6.cloned.1.call-done) | copy-start | bytes 786436
  193.2 99.7 %copy-start.4 = (f32[4,32,1024]{2,1,0:T(8,128)S(1)}, f32[4,32,1024]{2,1,0:T(8,128)}, u32[]{:S(2)}) copy-start(f32[4,32,1024]{2,1,0:T(8,128)} %param.8) | copy-start | bytes 1572868
  193.2 99.7 %copy-start.5 = (f32[4,32,1024]{2,1,0:T(8,128)S(1)}, f32[4,32,1024]{2,1,0:T(8,128)}, u32[]{:S(2)}) copy-start(f32[4,32,1024]{2,1,0:T(8,128)} %param.9) | copy-start | bytes 1572868
  193.2 99.7 %reduce-scatter.10.cloned.1.call-start = ((), (), s32[]{:S(2)}) async-start(), calls=%async_computation.8 | async-start | bytes 4456448
  212.1 143.3 %copy-start.6 = (f32[4,32,1024]{2,1,0:T(8,128)S(1)}, f32[4,32,1024]{2,1,0:T(8,128)}, u32[]{:S(2)}) copy-start(f32[4,32,1024]{2,1,0:T(8,128)} %param.7) | copy-start | bytes 1572868
  212.1 143.3 %all-gather.5.cloned.1.call-start = ((), (), s32[]{:S(2)}) async-start(), calls=%async_computation.7 | async-start | bytes 8650752 | tf_op jit(solution)/shard_map/all_gather | solution.py:76
  294.1 67.1 %copy-start.1 = (f32[4,32,1024]{2,1,0:T(8,128)}, f32[4,32,1024]{2,1,0:T(8,128)S(1)}, u32[]{:S(2)}) copy-start(f32[4,32,1024]{2,1,0:T(8,128)S(1)} %get-tuple-element.4) | copy-start | bytes 1572868
  294.1 67.1 %copy-start.2 = (f32[4,32,1024]{2,1,0:T(8,128)}, f32[4,32,1024]{2,1,0:T(8,128)S(1)}, u32[]{:S(2)}) copy-start(f32[4,32,1024]{2,1,0:T(8,128)S(1)} %get-tuple-element.5) | copy-start | bytes 1572868
Sparse Core Ops, SparseCore 0:
  11.7 94.0 reduce-scatter.5
  108.2 54.1 all-gather.2
  193.4 18.6 reduce-scatter.7
  215.3 77.5 reduce-scatter.9
  301.3 54.0 all-gather.4
